TPU v7x, 32 devices: a whole 2x2x4 slice. The times are simulated.
32 devices in a mesh: prow: 4 (over y, x), pcol: 8 (over z, core).
Axes of the slice: x: 2, y: 2, z: 4, core: 2. Of those that a mesh axis runs over, the one named last changes fastest.
Arguments:
- covariance: float32 [16384, 16384], P(('prow', 'pcol')), may hold values from -600 to 600, as said below
- factor_left: float32 [64, 16384], P(None, ('prow', 'pcol')), may hold values from -6 to 6
- factor_right: float32 [64, 16384], P('prow', 'pcol'), may hold values from -3 to 3
Outputs:
- whitened: float32 [16384, 16384], P('prow', 'pcol')
Inputs may be any that keep to these rules, and one draw needn't show every extreme that they name: `covariance`: entries are real-valued and of full rank.
All inputs are finite; a program needn't handle non-finite values.
Results may differ from a plain program's by a relative error of at most 0.00007.
Values sent between devices are 32-bit elements; how exact they have to be, the bound alone decides.
A program may use at most 192 MiB of HBM per device.

v0:
```python
import jax
import jax.numpy as jnp
from jax import lax
from jax.sharding import PartitionSpec as P

ORDER = 16384
TILE = 64
epsilon = 1e-06


def deal_columns(source):
    height = source.shape[0]
    breadth = source.shape[1]
    grid_cols = lax.axis_size("pcol")
    arranged = (
        source.reshape(height, breadth // (TILE * grid_cols), grid_cols, TILE)
        .transpose(0, 2, 1, 3)
        .reshape(height, breadth)
    )
    return lax.all_to_all(arranged, "pcol", split_axis=1, concat_axis=0, tiled=True)


def order_rows(source):
    height = source.shape[0]
    breadth = source.shape[1]
    grid_rows = lax.axis_size("prow")
    grouped = source.reshape(height // (TILE * grid_rows), grid_rows, TILE, breadth)
    return grouped.transpose(1, 0, 2, 3).reshape(height, breadth)


def body(covariance, factor_left, factor_right):
    right_panel = lax.all_gather(factor_right, "prow", axis=0, tiled=True)
    dealt = deal_columns(covariance)
    left_block = lax.all_gather(factor_left, "pcol", axis=1, tiled=True).T
    tiles_moved, left_rows = (
        lax.all_to_all(order_rows(dealt), "prow", split_axis=0, concat_axis=0, tiled=True),
        lax.all_to_all(order_rows(left_block), "prow", split_axis=0, concat_axis=0, tiled=True),
    )
    corrected = tiles_moved + jnp.dot(
        left_rows, right_panel, precision=lax.Precision.HIGHEST, preferred_element_type=jnp.float32
    )
    squared = corrected * corrected
    row_total = lax.psum(jnp.sum(squared, axis=1), "pcol")
    col_total = lax.psum(jnp.sum(squared, axis=0), "prow")
    row_mean = row_total / ORDER + epsilon
    col_mean = col_total / ORDER + epsilon
    return corrected * lax.rsqrt(jnp.sqrt(row_mean[:, None] * col_mean[None, :]))


def solution(mesh):
    placed = (P(("prow", "pcol"), None), P(None, ("prow", "pcol")), P("prow", "pcol"))
    return jax.shard_map(
        body, mesh=mesh, in_specs=placed, out_specs=P("prow", "pcol"), check_vma=False
    )
```

profile of v0, /device:TPU:0, one launch (start us, length us, event | category | flops | bytes accessed | tf_op | source)
XLA Modules:
  0.0 1344.6 jit_solution(4344010486472771985)
XLA Ops:
  6.5 33.4 %copy.8 = f32[512,16384]{0,1:T(8,128)} copy(f32[512,16384]{1,0:T(8,128)} %param.3) | data formatting | bytes 67108864 | tf_op args[0]
  40.0 23.8 %copy.9 = f32[512,8,32,64]{0,3,2,1:T(8,128)} copy(f32[512,8,32,64]{0,3,1,2:T(8,128)} %bitcast.28) | data formatting | bytes 67108864 | tf_op jit(solution)/shard_map/transpose | solution.py:17
  63.7 7.1 all-to-all-start
  70.8 0.0 all-gather.2.cloned.1.call-start
  70.8 0.7 all-gather.2.cloned.1.call-update
  71.5 36.2 %all-gather.2.cloned.1.call-done = f32[64,4096]{1,0:T(8,128)} async-done(((f32[64,512]{1,0:T(8,128)}), f32[64,4096]{1,0:T(8,128)}) %all-gather.2.cloned.1.call-update) | async-done | bytes 1048592 | tf_op jit(solution)/shard_map/all_gather | solution.py:34
  107.8 2.6 reshape.27
  110.4 1.5 copy.16
  111.9 2.8 all_to_all.34
  114.6 688.7 %all-to-all-done = f32[512,8,2048]{0,2,1:T(8,128)} async-done(((f32[512,8,2048]{0,2,1:T(8,128)}), f32[512,8,2048]{0,2,1:T(8,128)}, u32[]{:S(2)}, u32[]{:S(2)}) %all-to-all-start) | async-done | bytes 33554464 | tf_op jit(solution)/shard_map/all_to_all | solution.py:20
  803.3 4.3 all-to-all-start.2
  807.6 31.7 %copy.10 = f32[8,512,2048]{2,1,0:T(8,128)} copy(f32[8,512,2048]{1,2,0:T(8,128)} %bitcast.3) | data formatting | bytes 67108864 | tf_op jit(solution)/shard_map/all_to_all | solution.py:20
  839.3 23.0 %copy.11 = f32[4,16,64,2048]{3,2,1,0:T(8,128)} copy(f32[4,16,64,2048]{3,2,0,1:T(8,128)} %bitcast.27) | data formatting | bytes 67108864 | tf_op jit(solution)/shard_map/transpose | solution.py:28
  862.3 0.0 all-to-all-done.2
  862.3 0.0 copy-start
  862.3 9.8 all-to-all-start.1
  872.1 0.0 copy-done
  872.2 367.5 %all_gather.7 = f32[64,2048]{1,0:T(8,128)S(1)} all-gather(f32[16,2048]{1,0:T(8,128)S(1)} %copy-done), channel_id=1, replica_groups=mesh['prow'=4,'pcol'=8] {'prow'}, dimensions={0}, use_global_device_ids=true | all-gather | bytes 655360 | tf_op jit(solution)/shard_map/all_gather | solution.py:32
  1239.6 0.1 copy.14
  1239.8 0.0 all-to-all-done.1
  1239.8 35.9 %multiply_reduce_fusion.1 = (f32[4096]{0:T(1024)S(1)}, f32[2048]{0:T(1024)S(1)}, f32[4096,2048]{1,0:T(8,128)}) fusion(f32[4096,64]{0,1:T(8,128)S(1)} %bitcast.30, f32[64,2048]{1,0:T(8,128)S(1)} %all_gather.7, f32[4,1024,2048]{2,1,0:T(8,128)} %all-to-all-done.1), kind=kOutput, calls=%fused_computation.3 | convolution fusion | flops 6475999232 | bytes 68706304 | tf_op jit(solution)/shard_map/dot_general | solution.py:39
  1275.6 25.9 %psum.14 = f32[4096]{0:T(1024)S(1)} all-reduce(f32[4096]{0:T(1024)S(1)} %get-tuple-element.5), channel_id=1, replica_groups=mesh['prow'=4,'pcol'=8] {'pcol'}, use_global_device_ids=true, to_apply=%region_1.0 | all-reduce | flops 4096 | bytes 32768 | tf_op jit(solution)/shard_map/psum | solution.py:43
  1301.5 9.1 psum.15
  1310.6 27.1 %rsqrt_multiply_fusion = f32[4096,2048]{1,0:T(8,128)} fusion(f32[4096,2048]{1,0:T(8,128)} %get-tuple-element.7, f32[2048]{0:T(1024)S(1)} %multiply_add_fusion.1, f32[4096]{0:T(1024)S(1)} %multiply_add_fusion), kind=kLoop, calls=%fused_computation.1 | loop fusion | flops 16777216 | bytes 67133440 | tf_op jit(solution)/shard_map/mul | solution.py:47
  (2 shorter events, 0.0 us)
Async XLA Ops:
  63.7 739.5 %all-to-all-start = ((f32[512,8,2048]{0,2,1:T(8,128)}), f32[512,8,2048]{0,2,1:T(8,128)}, u32[]{:S(2)}, u32[]{:S(2)}) async-start(f32[512,8,2048]{0,2,1:T(8,128)} %bitcast.25), calls=%async_computation | async-start | bytes 67108864 | tf_op jit(solution)/shard_map/all_to_all | solution.py:20
  70.8 36.9 %all-gather.2.cloned.1.call-start = ((), (), s32[]{:S(2)}) async-start(), calls=%async_computation.3 | async-start | bytes 1179648 | tf_op jit(solution)/shard_map/all_gather | solution.py:34
  803.3 59.0 %all-to-all-start.2 = ((f32[4,1024,64]{1,2,0:T(8,128)}), f32[4,1024,64]{1,2,0:T(8,128)S(1)}, u32[]{:S(2)}, u32[]{:S(2)}) async-start(f32[4,1024,64]{1,2,0:T(8,128)} %all_to_all.34), calls=%async_computation.2 | async-start | bytes 2097152 | tf_op jit(solution)/shard_map/all_to_all | solution.py:37
  862.3 9.8 copy-start
  862.3 377.4 %all-to-all-start.1 = ((f32[4,1024,2048]{2,1,0:T(8,128)}), f32[4,1024,2048]{2,1,0:T(8,128)}, u32[]{:S(2)}, u32[]{:S(2)}) async-start(f32[4,1024,2048]{2,1,0:T(8,128)} %bitcast.26), calls=%async_computation.1 | async-start | bytes 67108864 | tf_op jit(solution)/shard_map/all_to_all | solution.py:36
Sparse Core Ops, SparseCore 0:
  73.2 34.4 all-gather.1
where the time goes:
time: 1350 us; the launch traced here: 1340 us
  waiting for transfers between devices  726 us (54%)
  blocking collectives  402 us (30%)
  local copies, waits for them, and re-layouts  119 us (9%)
  matrix products  35.9 us (3%)
  other arithmetic  27.1 us (2%)
  starting transfers between devices  21.2 us (2%)
  between operations  13.5 us (1%)
    all_to_all x1, waiting for transfers between devices, deal_columns(): lax.all_to_all(arranged, 'pcol', split_axis=1, concat_axis=0, tiled=True)  689 us
    all_gather x1, blocking collectives, body(): right_panel = lax.all_gather(factor_right, 'prow', axis=0, tiled=True)  367 us
    all_gather x1, waiting for transfers between devices, body(): left_block = lax.all_gather(factor_left, 'pcol', axis=1, tiled=True).T  36.2 us
    dot_general x1, matrix products, body(): jnp.dot(left_rows, right_panel, precision=lax.Precision.HIGHEST, preferre...  35.9 us
    unnamed x3, local copies, waits for them, and re-layouts  33.4 us
    all_to_all x1, local copies, waits for them, and re-layouts, deal_columns(): lax.all_to_all(arranged, 'pcol', split_axis=1, concat_axis=0, tiled=True)  31.7 us
    mul x1, other arithmetic, body(): corrected * lax.rsqrt(jnp.sqrt(row_mean[:, None] * col_mean[None, :]))  27.1 us
  transfers between devices with their start and end apart: 4, of which 2 were waited for; matrix products, arithmetic and copies ran while one was open for 4% of the time, Pallas kernels for 0%

commit v1 on v0

--- a/solution.py
+++ b/solution.py
@@ -29,7 +29,12 @@
 
 
 def body(covariance, factor_left, factor_right):
-    right_panel = lax.all_gather(factor_right, "prow", axis=0, tiled=True)
+    ring = [factor_right]
+    for hop in range(3):
+        ring.append(lax.ppermute(ring[-1], "prow", [(dev, (dev + 1) % 4) for dev in range(4)]))
+    right_panel = jnp.roll(
+        jnp.concatenate(ring[::-1], axis=0), (lax.axis_index("prow") + 1) * ring[0].shape[0], axis=0
+    )
     dealt = deal_columns(covariance)
     left_block = lax.all_gather(factor_left, "pcol", axis=1, tiled=True).T
     tiles_moved, left_rows = (

time: 1350 us -> 1420 us (1.052)
  waiting for transfers between devices: 726 us -> 1100 us
  blocking collectives: 402 us -> 33.5 us
  local copies, waits for them, and re-layouts: 119 us -> 183 us
    ppermute x0 -> x3, waiting for transfers between devices: none -> 375 us  [body(): lax.ppermute(ring[-1], 'prow', [(dev, (dev + 1) % 4) for dev in range(4)])]
    all_gather x1 -> x0, blocking collectives: 367 us -> none  [body(): right_panel = lax.all_gather(factor_right, 'prow', axis=0, tiled=True)]
    mul x0 -> x1, local copies, waits for them, and re-layouts: none -> 33.3 us  [body(): corrected * lax.rsqrt(jnp.sqrt(row_mean[:, None] * col_mean[None, :]))]
    all_to_all x0 -> x1, local copies, waits for them, and re-layouts: none -> 31.1 us  [body(): lax.all_to_all(order_rows(dealt), 'prow', split_axis=0, concat_axis=0, ti...]
    unnamed x3 -> x10, local copies, waits for them, and re-layouts: 33.4 us -> 33.5 us
  transfers between devices with their start and end apart: 4 -> 7, of which waited for: 2 -> 5; matrix products, arithmetic and copies ran while one was open for 4% -> 4% of each run, Pallas kernels for 0% -> 0%
where the time goes in v1:
time: 1420 us
  waiting for transfers between devices  1100 us (77%)
  local copies, waits for them, and re-layouts  183 us (13%)
  matrix products  36 us (3%)
  blocking collectives  33.5 us (2%)
  other arithmetic  26.6 us (2%)
  starting transfers between devices  23.3 us (2%)
    all_to_all x1, waiting for transfers between devices, deal_columns(): lax.all_to_all(arranged, 'pcol', split_axis=1, concat_axis=0, tiled=True)  689 us
    ppermute x3, waiting for transfers between devices, body(): lax.ppermute(ring[-1], 'prow', [(dev, (dev + 1) % 4) for dev in range(4)])  375 us
    all_gather x1, waiting for transfers between devices, body(): left_block = lax.all_gather(factor_left, 'pcol', axis=1, tiled=True).T  36.2 us
    dot_general x1, matrix products, body(): jnp.dot(left_rows, right_panel, precision=lax.Precision.HIGHEST, preferre...  36 us
    unnamed x10, local copies, waits for them, and re-layouts  33.5 us
    mul x1, local copies, waits for them, and re-layouts, body(): corrected * lax.rsqrt(jnp.sqrt(row_mean[:, None] * col_mean[None, :]))  33.3 us
    all_to_all x1, local copies, waits for them, and re-layouts, deal_columns(): lax.all_to_all(arranged, 'pcol', split_axis=1, concat_axis=0, tiled=True)  31.7 us
    all_to_all x1, local copies, waits for them, and re-layouts, body(): lax.all_to_all(order_rows(dealt), 'prow', split_axis=0, concat_axis=0, ti...  31.1 us
  transfers between devices with their start and end apart: 7, of which 5 were waited for; matrix products, arithmetic and copies ran while one was open for 4% of the time, Pallas kernels for 0%

profile of v1, /device:TPU:0, one launch (start us, length us, event | category | flops | bytes accessed | tf_op | source)
XLA Modules:
  0.0 1416.9 jit_solution(12684092029813159158)
XLA Ops:
  6.5 33.4 %copy.12 = f32[512,16384]{0,1:T(8,128)} copy(f32[512,16384]{1,0:T(8,128)} %param.3) | data formatting | bytes 67108864 | tf_op args[0]
  40.0 23.8 %copy.13 = f32[512,8,32,64]{0,3,2,1:T(8,128)} copy(f32[512,8,32,64]{0,3,1,2:T(8,128)} %bitcast.28) | data formatting | bytes 67108864 | tf_op jit(solution)/shard_map/transpose | solution.py:17
  63.7 7.1 all-to-all-start
  70.8 0.0 all-gather.2.cloned.1.call-start
  70.9 0.7 all-gather.2.cloned.1.call-update
  71.5 36.2 %all-gather.2.cloned.1.call-done = f32[64,4096]{1,0:T(8,128)} async-done(((f32[64,512]{1,0:T(8,128)}), f32[64,4096]{1,0:T(8,128)}) %all-gather.2.cloned.1.call-update) | async-done | bytes 1048592 | tf_op jit(solution)/shard_map/all_gather | solution.py:39
  107.8 2.6 reshape.27
  110.4 1.5 copy.23
  111.9 2.8 all_to_all.34
  114.6 688.6 %all-to-all-done = f32[512,8,2048]{0,2,1:T(8,128)} async-done(((f32[512,8,2048]{0,2,1:T(8,128)}), f32[512,8,2048]{0,2,1:T(8,128)}, u32[]{:S(2)}, u32[]{:S(2)}) %all-to-all-start) | async-done | bytes 33554464 | tf_op jit(solution)/shard_map/all_to_all | solution.py:20
  803.3 4.3 all-to-all-start.2
  807.6 31.7 %copy.14 = f32[8,512,2048]{2,1,0:T(8,128)} copy(f32[8,512,2048]{1,2,0:T(8,128)} %bitcast.3) | data formatting | bytes 67108864 | tf_op jit(solution)/shard_map/all_to_all | solution.py:20
  839.3 23.0 %copy.15 = f32[4,16,64,2048]{3,2,1,0:T(8,128)} copy(f32[4,16,64,2048]{3,2,0,1:T(8,128)} %bitcast.27) | data formatting | bytes 67108864 | tf_op jit(solution)/shard_map/transpose | solution.py:28
  862.3 0.0 all-to-all-done.2
  862.3 0.0 copy-start
  862.3 9.8 all-to-all-start.1
  872.2 0.0 copy-done
  872.2 2.1 collective-permute-start
  874.2 363.2 %collective-permute-done = f32[16,2048]{1,0:T(8,128)S(1)} collective-permute-done((f32[16,2048]{1,0:T(8,128)S(1)}, f32[16,2048]{1,0:T(8,128)S(1)}, u32[]{:S(2)}, u32[]{:S(2)}) %collective-permute-start) | collective-permute-done | bytes 131104 | tf_op jit(solution)/shard_map/ppermute | solution.py:34
  1237.5 0.0 collective-permute-start.1
  1237.5 5.9 collective-permute-done.1
  1243.3 0.0 collective-permute-start.2
  1243.4 5.9 collective-permute-done.2
  1249.4 0.1 copy.21
  1249.5 0.0 all-to-all-done.1
  1249.5 31.1 %copy.20 = f32[4096,2048]{0,1:T(8,128)} copy(f32[4096,2048]{1,0:T(8,128)} %bitcast.7) | data formatting | bytes 67108864 | tf_op jit(solution)/shard_map/all_to_all | solution.py:41
  1280.6 36.0 %multiply_reduce_fusion.1 = (f32[4096]{0:T(1024)S(1)}, f32[2048]{0:T(1024)S(1)}, f32[4096,2048]{0,1:T(8,128)}) fusion(f32[4096,2048]{0,1:T(8,128)} %copy.20, f32[4096,64]{0,1:T(8,128)S(1)} %bitcast.30, f32[128,2048]{1,0:T(8,128)S(1)} %constant_dynamic-update-slice_fusion, s32[]{:T(128)S(6)} %select_n.14), kind=kOutput, calls=%fused_computation.3 | convolution fusion | flops 6475999232 | bytes 68706304 | tf_op jit(solution)/shard_map/dot_general | solution.py:44
  1316.6 7.6 psum.15
  1324.2 25.9 %psum.14 = f32[4096]{0:T(1024)S(1)} all-reduce(f32[4096]{0:T(1024)S(1)} %get-tuple-element.5), channel_id=1, replica_groups=mesh['prow'=4,'pcol'=8] {'pcol'}, use_global_device_ids=true, to_apply=%region_1.2 | all-reduce | flops 4096 | bytes 32768 | tf_op jit(solution)/shard_map/psum | solution.py:48
  1350.1 26.6 %rsqrt_multiply_fusion = f32[4096,2048]{0,1:T(8,128)} fusion(f32[4096,2048]{0,1:T(8,128)} %get-tuple-element.7, f32[2048]{0:T(1024)S(1)} %multiply_add_fusion.1, f32[4096]{0:T(1024)S(1)} %multiply_add_fusion), kind=kLoop, calls=%fused_computation.1 | loop fusion | flops 16777216 | bytes 67133440 | tf_op jit(solution)/shard_map/mul | solution.py:52
  1376.7 33.3 %copy.19 = f32[4096,2048]{1,0:T(8,128)} copy(f32[4096,2048]{0,1:T(8,128)} %rsqrt_multiply_fusion) | data formatting | bytes 67108864 | tf_op jit(solution)/shard_map/mul | solution.py:52
  (10 shorter events, 0.1 us)
Async XLA Ops:
  63.7 739.6 %all-to-all-start = ((f32[512,8,2048]{0,2,1:T(8,128)}), f32[512,8,2048]{0,2,1:T(8,128)}, u32[]{:S(2)}, u32[]{:S(2)}) async-start(f32[512,8,2048]{0,2,1:T(8,128)} %bitcast.26), calls=%async_computation | async-start | bytes 67108864 | tf_op jit(solution)/shard_map/all_to_all | solution.py:20
  70.8 37.0 %all-gather.2.cloned.1.call-start = ((), (), s32[]{:S(2)}) async-start(), calls=%async_computation.3 | async-start | bytes 1179648 | tf_op jit(solution)/shard_map/all_gather | solution.py:39
  803.3 59.0 %all-to-all-start.2 = ((f32[4,1024,64]{1,2,0:T(8,128)}), f32[4,1024,64]{1,2,0:T(8,128)S(1)}, u32[]{:S(2)}, u32[]{:S(2)}) async-start(f32[4,1024,64]{1,2,0:T(8,128)} %all_to_all.34), calls=%async_computation.2 | async-start | bytes 2097152 | tf_op jit(solution)/shard_map/all_to_all | solution.py:42
  862.3 9.8 copy-start
  862.3 387.1 %all-to-all-start.1 = ((f32[4,1024,2048]{2,1,0:T(8,128)}), f32[4,1024,2048]{2,1,0:T(8,128)}, u32[]{:S(2)}, u32[]{:S(2)}) async-start(f32[4,1024,2048]{2,1,0:T(8,128)} %bitcast.25), calls=%async_computation.1 | async-start | bytes 67108864 | tf_op jit(solution)/shard_map/all_to_all | solution.py:41
  872.2 365.3 %collective-permute-start = (f32[16,2048]{1,0:T(8,128)S(1)}, f32[16,2048]{1,0:T(8,128)S(1)}, u32[]{:S(2)}, u32[]{:S(2)}) collective-permute-start(f32[16,2048]{1,0:T(8,128)S(1)} %copy-done), channel_id=1, source_target_pairs={{0,8},{8,16},{16,24},{24,0},{1,9},{9,17},{17,25},{25,1},{2,10},{10... | collective-permute-start | bytes 393224 | tf_op jit(solution)/shard_map/ppermute | solution.py:34
  1237.5 5.9 collective-permute-start.1
  1243.3 5.9 collective-permute-start.2
Sparse Core Ops, SparseCore 0:
  73.2 34.4 all-gather.1
